TPU v7x, 32 devices: a whole 2x2x4 slice. The times are simulated.
32 devices in a mesh: grp: 2 (over x), freq: 16 (over z, y, core).
Axes of the slice: x: 2, y: 2, z: 4, core: 2. Of those that a mesh axis runs over, the one named last changes fastest.
Arguments:
- kernel: bfloat16 [2, 256, 1024, 1024], P(None, ('grp', 'freq')), parts along dimension 1, may hold values from -0.125 to 0.125
- recorded: float32 [2, 256, 1024, 128], P(None, ('grp', 'freq')), parts along dimension 1, may hold values from -8 to 8
- onset_time: int32 [2048, 128], P(('grp', 'freq')), parts along dimension 0, may hold values from 32 to 256, as said below
Outputs:
- focusing: float32 [256, 2048, 128], P(None, ('grp', 'freq')), parts along dimension 1
There are 2 independent parts, one for each index of `grp`. A program takes and returns all parts, laid end to end along the dimension named above; each array names one. Nothing has to cross between parts.
Inputs may be any that keep to these rules, and one draw needn't show every extreme that they name: `onset_time`: onset sample of the window for each receiver and focal point.
All inputs are finite; a program needn't handle non-finite values.
Results may differ from a plain program's by a relative error of at most 0.012.
Values may be sent and summed in bfloat16 or wider, within the bound.
A program may use at most 192 MiB of HBM per device.

v0:
```python
import math
import jax
import jax.numpy as jnp
from jax import lax
from jax.sharding import PartitionSpec as P

NF = 128
ITERS = 2


def dft_tables():
    samples = jnp.arange(2 * NF, dtype=jnp.int32)
    bins = jnp.arange(NF, dtype=jnp.int32)
    phase = (bins[:, None] * samples[None, :] % (2 * NF)).astype(jnp.float32) * (math.pi / NF)
    factor = 1.0 / math.sqrt(NF)
    return (jnp.cos(phase) * factor, jnp.sin(phase) * factor)


def square_sum(values):
    return jnp.sum(values * values)


def joint_total(first, second, third):
    return lax.psum((first, second, third), "freq")


def body(kernel, recorded, onset_time):
    highest = lax.Precision.HIGHEST
    cosine_table, sin_tab = dft_tables()
    rec_local = onset_time.shape[0]
    focal_count = onset_time.shape[1]
    samples = lax.broadcasted_iota(jnp.int32, (2 * NF, rec_local, focal_count), 0)
    keep_mask = (samples < onset_time[None]).astype(jnp.float32)
    kernel_real = kernel[0]
    kernel_imaginary = kernel[1]

    def invert(block_in):
        columns = block_in.shape[3]
        widened = block_in.astype(jnp.float32)
        timed = jnp.dot(cosine_table.T, widened[0].reshape(NF, -1), precision=highest) - jnp.dot(
            sin_tab.T, widened[1].reshape(NF, -1), precision=highest
        )
        return timed.reshape(2 * NF, block_in.shape[2], columns)

    def apply_adjoint(resid):
        rounded = resid.astype(jnp.bfloat16)
        update_real = rounded[0]
        update_imaginary = rounded[1]
        z_real = jnp.einsum(
            "hvi,hvg->hig", kernel_real, update_real, preferred_element_type=jnp.float32
        ) + jnp.einsum(
            "hvi,hvg->hig", kernel_imaginary, update_imaginary, preferred_element_type=jnp.float32
        )
        z_imag = jnp.einsum(
            "hvi,hvg->hig", kernel_real, update_imaginary, preferred_element_type=jnp.float32
        ) - jnp.einsum(
            "hvi,hvg->hig", kernel_imaginary, update_real, preferred_element_type=jnp.float32
        )
        image = jnp.stack([z_real, z_imag]).astype(jnp.bfloat16)
        timed = invert(lax.all_to_all(image, "freq", split_axis=2, concat_axis=1, tiled=True))
        return timed * keep_mask

    model_raw = apply_adjoint(recorded)
    totals = joint_total(square_sum(recorded), square_sum(model_raw), jnp.float32(0.0))
    beta_now = jnp.sqrt(totals[0])
    data_vec = recorded / beta_now
    alpha_now = jnp.sqrt(totals[1]) / beta_now
    model_vec = model_raw / (alpha_now * beta_now)
    search = model_vec
    estimate = jnp.zeros_like(model_vec)
    phibar_now = beta_now
    rhobar_now = alpha_now
    for iteration in range(ITERS):
        flat_part = (model_vec * keep_mask).reshape(2 * NF, -1)
        spec_real = jnp.dot(cosine_table, flat_part, precision=highest)
        spec_imag = -jnp.dot(sin_tab, flat_part, precision=highest)
        spectrum = (
            jnp.stack([spec_real, spec_imag])
            .reshape(2, NF, rec_local, focal_count)
            .astype(jnp.bfloat16)
        )
        multiply_block_in = lax.all_to_all(
            spectrum, "freq", split_axis=1, concat_axis=2, tiled=True
        )
        solution_real = multiply_block_in[0]
        solution_imaginary = multiply_block_in[1]
        y_real = jnp.einsum(
            "ptx,pxi->pti", kernel_real, solution_real, preferred_element_type=jnp.float32
        ) - jnp.einsum(
            "ptx,pxi->pti", kernel_imaginary, solution_imaginary, preferred_element_type=jnp.float32
        )
        y_imag = jnp.einsum(
            "ptx,pxi->pti", kernel_real, solution_imaginary, preferred_element_type=jnp.float32
        ) + jnp.einsum(
            "ptx,pxi->pti", kernel_imaginary, solution_real, preferred_element_type=jnp.float32
        )
        data_raw = jnp.stack([y_real, y_imag]) - alpha_now * data_vec
        image_raw = apply_adjoint(data_raw)
        totals = joint_total(
            square_sum(data_raw), square_sum(image_raw), jnp.sum(image_raw * model_vec)
        )
        beta_now = jnp.sqrt(totals[0])
        data_vec = data_raw / beta_now
        alpha_now = jnp.sqrt(
            totals[1] / (beta_now * beta_now) - 2.0 * totals[2] + beta_now * beta_now
        )
        model_vec = (image_raw / beta_now - beta_now * model_vec) / alpha_now
        rho_now = jnp.sqrt(rhobar_now * rhobar_now + beta_now * beta_now)
        cosine = rhobar_now / rho_now
        sine_part = beta_now / rho_now
        theta_now = sine_part * alpha_now
        rhobar_now = -cosine * alpha_now
        phi_now = cosine * phibar_now
        phibar_now = sine_part * phibar_now
        estimate = estimate + phi_now / rho_now * search
        search = model_vec - theta_now / rho_now * search
    return estimate


def solution(mesh):
    placed = (
        P(None, ("grp", "freq"), None, None),
        P(None, ("grp", "freq"), None, None),
        P(("grp", "freq"), None),
    )
    return jax.shard_map(
        body, mesh=mesh, in_specs=placed, out_specs=P(None, ("grp", "freq"), None), check_vma=False
    )
```

profile of v0, /device:TPU:0, one launch (start us, length us, event | category | flops | bytes accessed | tf_op | source)
XLA Modules:
  0.0 832.4 jit_solution(1631037788863570241)
XLA Ops:
  8.5 10.8 %fusion.14 = f32[8,1024,128]{2,1,0:T(8,128)} fusion(bf16[2,8,1024,1024]{3,2,1,0:T(8,128)(2,1)} %param.3, bf16[2,8,1024,128]{3,2,1,0:T(8,128)(2,1)S(1)} %get-tuple-element.15), kind=kOutput, calls=%fused_computation.14 | convolution fusion | flops 2147483648 | bytes 23068672 | tf_op jit(solution)/shard_map/hvi,hvg->hig/dot_general | solution.py:51
  19.4 10.7 %fusion.12 = f32[8,1024,128]{2,1,0:T(8,128)} fusion(bf16[2,8,1024,1024]{3,2,1,0:T(8,128)(2,1)} %param.3, bf16[2,8,1024,128]{3,2,1,0:T(8,128)(2,1)S(1)} %get-tuple-element.15), kind=kOutput, calls=%fused_computation.12 | convolution fusion | flops 2147483648 | bytes 23068672 | tf_op jit(solution)/shard_map/hvi,hvg->hig/dot_general | solution.py:56
  39.7 10.4 %fusion.68 = bf16[1,8,1024,128]{3,2,1,0:T(8,128)(2,1)S(1)} fusion(f32[8,1024,128]{2,1,0:T(8,128)} %fusion.12, bf16[2,8,1024,128]{3,2,1,0:T(8,128)(2,1)S(1)} %get-tuple-element.15, bf16[2,8,1024,1024]{3,2,1,0:T(8,128)(2,1)} %param.3), kind=kOutput, calls=%fused_computation.98 | convolution fusion | flops 2149580800 | bytes 25165824 | tf_op jit(solution)/shard_map/hvi,hvg->hig/dot_general | solution.py:54
  53.2 99.3 %all_to_all.60 = bf16[2,8,1024,128]{3,1,0,2:T(8,128)(2,1)S(1)} all-to-all(bf16[2,8,1024,128]{3,1,0,2:T(8,128)(2,1)S(1)} %copy.81), channel_id=1, replica_groups=mesh['grp'=2,'freq'=16] {'freq'}, dimensions={2} | all-to-all | bytes 8388608 | tf_op jit(solution)/shard_map/all_to_all | solution.py:60
  159.0 12.1 %multiply_reduce_fusion.4 = (f32[]{:T(128)}, f32[256,8192]{1,0:T(8,128)}) fusion(s32[8192]{0:T(1024)S(1)} %bitcast.250, f32[256,8192]{1,0:T(8,128)S(1)} %fusion.78, bf16[16,8,64,128]{3,2,1,0:T(8,128)(2,1)S(1)} %get-tuple-element.22), kind=kOutput, calls=%fused_computation.58 | convolution fusion | flops 3232202752 | bytes 18907140 | tf_op jit(solution)/shard_map/dot_general | solution.py:40
  171.1 34.1 %all-reduce.1 = (f32[]{:T(128)}, f32[]{:T(128)}) all-reduce(f32[]{:T(128)} %get-tuple-element.24, f32[]{:T(128)} %get-tuple-element.14), channel_id=1, replica_groups=mesh['grp'=2,'freq'=16] {'freq'}, use_global_device_ids=true, to_apply=%region_1.2 | all-reduce | flops 2 | bytes 16 | tf_op jit(solution)/shard_map/psum | solution.py:24
  206.5 10.7 %fusion.89 = bf16[16,8,64,128]{3,1,2,0:T(8,128)(2,1)S(1)} fusion(s32[8192]{0:T(1024)S(1)} %bitcast.251, f32[256,8192]{1,0:T(8,128)} %get-tuple-element.25, f32[]{:T(128)S(6)} %mul.210), kind=kOutput, calls=%fused_computation.123 | convolution fusion | flops 3231154176 | bytes 10518532 | tf_op jit(solution)/shard_map/dot_general | solution.py:75
  242.5 68.8 %all-to-all-done.1 = bf16[2,128,64,128]{3,2,0,1:T(8,128)(2,1)} async-done(((bf16[2,128,64,128]{3,2,0,1:T(8,128)(2,1)}), bf16[2,128,64,128]{3,2,0,1:T(8,128)(2,1)}, u32[]{:S(2)}, u32[]{:S(2)}) %all-to-all-start.1) | async-done | bytes 4194336 | tf_op jit(solution)/shard_map/all_to_all | solution.py:82
  316.9 14.0 %fusion.10 = f32[8,128,1024]{2,1,0:T(8,128)} fusion(bf16[8,1024,128]{2,1,0:T(8,128)(2,1)} %bitcast.241, bf16[2,8,1024,1024]{3,2,1,0:T(8,128)(2,1)} %param.3), kind=kOutput, calls=%fused_computation.10 | convolution fusion | flops 2147483648 | bytes 23068672 | tf_op jit(solution)/shard_map/ptx,pxi->pti/dot_general | solution.py:89
  332.5 14.0 %fusion.8 = f32[8,128,1024]{2,1,0:T(8,128)} fusion(bf16[8,1024,128]{2,1,0:T(8,128)(2,1)} %bitcast.246, bf16[2,8,1024,1024]{3,2,1,0:T(8,128)(2,1)} %param.3), kind=kOutput, calls=%fused_computation.8 | convolution fusion | flops 2147483648 | bytes 23068672 | tf_op jit(solution)/shard_map/ptx,pxi->pti/dot_general | solution.py:94
  346.5 10.8 %subtract_bitcast_fusion.1 = f32[1,8,1024,128]{2,3,1,0:T(8,128)S(1)} fusion(f32[8,128,1024]{2,1,0:T(8,128)} %fusion.10, bf16[8,1024,128]{2,1,0:T(8,128)(2,1)} %bitcast.247, bf16[2,8,1024,1024]{3,2,1,0:T(8,128)(2,1)} %param.3), kind=kOutput, calls=%fused_computation.74 | convolution fusion | flops 2148532224 | bytes 27262976 | tf_op jit(solution)/shard_map/ptx,pxi->pti/dot_general | solution.py:87
  357.3 11.2 %add_bitcast_fusion.1 = f32[1,8,1024,128]{2,3,1,0:T(8,128)} fusion(f32[8,128,1024]{2,1,0:T(8,128)} %fusion.8, bf16[8,1024,128]{2,1,0:T(8,128)(2,1)S(1)} %bitcast.242, bf16[2,8,1024,1024]{3,2,1,0:T(8,128)(2,1)} %param.3), kind=kOutput, calls=%fused_computation.73 | convolution fusion | flops 2148532224 | bytes 27262976 | tf_op jit(solution)/shard_map/ptx,pxi->pti/dot_general | solution.py:92
  378.8 10.1 %fusion.6 = f32[8,128,1024]{2,1,0:T(8,128)} fusion(bf16[2,8,1024,1024]{3,2,1,0:T(8,128)(2,1)} %param.3, bf16[2,8,1024,128]{2,3,1,0:T(8,128)(2,1)S(1)} %convert_element_type.32), kind=kOutput, calls=%fused_computation.6 | convolution fusion | flops 2147483648 | bytes 23068672 | tf_op jit(solution)/shard_map/hvi,hvg->hig/dot_general | solution.py:51
  388.9 10.1 %fusion.4 = f32[8,128,1024]{2,1,0:T(8,128)} fusion(bf16[2,8,1024,1024]{3,2,1,0:T(8,128)(2,1)} %param.3, bf16[2,8,1024,128]{2,3,1,0:T(8,128)(2,1)S(1)} %convert_element_type.32), kind=kOutput, calls=%fused_computation.4 | convolution fusion | flops 2147483648 | bytes 23068672 | tf_op jit(solution)/shard_map/hvi,hvg->hig/dot_general | solution.py:56
  408.5 10.8 %fusion.70 = bf16[1,8,1024,128]{2,3,1,0:T(8,128)(2,1)} fusion(f32[8,128,1024]{2,1,0:T(8,128)} %fusion.4, bf16[2,8,1024,1024]{3,2,1,0:T(8,128)(2,1)} %param.3, bf16[2,8,1024,128]{2,3,1,0:T(8,128)(2,1)S(1)} %convert_element_type.32), kind=kOutput, calls=%fused_computation.100 | convolution fusion | flops 2149580800 | bytes 25165824 | tf_op jit(solution)/shard_map/hvi,hvg->hig/dot_general | solution.py:54
  430.2 112.1 %all_to_all.61 = bf16[2,8,1024,128]{3,1,0,2:T(8,128)(2,1)S(1)} all-to-all(bf16[2,8,1024,128]{3,1,0,2:T(8,128)(2,1)} %copy.101), channel_id=1, replica_groups=mesh['grp'=2,'freq'=16] {'freq'}, dimensions={2} | all-to-all | bytes 8388608 | tf_op jit(solution)/shard_map/all_to_all | solution.py:60
  549.1 11.3 %multiply_reduce_fusion = (f32[]{:T(128)}, f32[]{:T(128)}, f32[256,8192]{1,0:T(8,128)}) fusion(s32[8192]{0:T(1024)S(1)} %bitcast.253, f32[]{:T(128)S(6)} %mul.210, f32[256,8192]{1,0:T(8,128)S(1)} %bitcast.229, f32[256,8192]{1,0:T(8,128)S(1)} %fusion.73, bf16[16,8,64,128]{3,2,1,0:T(8,128)(2,1)S(1)} %bitcast.245), kind=kOutput, calls=%fused_computation.53 | convolution fusion | flops 3240591360 | bytes 27295756 | tf_op jit(solution)/shard_map/dot_general | solution.py:40
  560.4 34.2 %all-reduce = (f32[]{:T(128)}, f32[]{:T(128)}, f32[]{:T(128)}) all-reduce(f32[]{:T(128)} %get-tuple-element.12, f32[]{:T(128)} %get-tuple-element.6, f32[]{:T(128)} %get-tuple-element.5), channel_id=1, replica_groups=mesh['grp'=2,'freq'=16] {'freq'}, use_global_device_ids=true, to_apply=%region_5.6 | all-reduce | flops 3 | bytes 24 | tf_op jit(solution)/shard_map/psum | solution.py:24
  632.4 68.8 %all-to-all-done.3 = bf16[2,128,64,128]{3,2,0,1:T(8,128)(2,1)} async-done(((bf16[2,128,64,128]{3,2,0,1:T(8,128)(2,1)}), bf16[2,128,64,128]{3,2,0,1:T(8,128)(2,1)}, u32[]{:S(2)}, u32[]{:S(2)}) %all-to-all-start.3) | async-done | bytes 4194336 | tf_op jit(solution)/shard_map/all_to_all | solution.py:82
  706.8 14.0 %fusion.2 = f32[8,128,1024]{2,1,0:T(8,128)} fusion(bf16[8,1024,128]{2,1,0:T(8,128)(2,1)} %bitcast.243, bf16[2,8,1024,1024]{3,2,1,0:T(8,128)(2,1)} %param.3), kind=kOutput, calls=%fused_computation.2 | convolution fusion | flops 2147483648 | bytes 23068672 | tf_op jit(solution)/shard_map/ptx,pxi->pti/dot_general | solution.py:89
  722.4 14.3 %fusion = f32[8,128,1024]{2,1,0:T(8,128)} fusion(bf16[8,1024,128]{2,1,0:T(8,128)(2,1)} %bitcast.248, bf16[2,8,1024,1024]{3,2,1,0:T(8,128)(2,1)} %param.3), kind=kOutput, calls=%fused_computation | convolution fusion | flops 2147483648 | bytes 23068672 | tf_op jit(solution)/shard_map/ptx,pxi->pti/dot_general | solution.py:94
  736.8 10.7 %subtract_bitcast_fusion = f32[1,8,1024,128]{2,3,1,0:T(8,128)S(1)} fusion(f32[8,128,1024]{2,1,0:T(8,128)} %fusion.2, bf16[8,1024,128]{2,1,0:T(8,128)(2,1)} %bitcast.249, bf16[2,8,1024,1024]{3,2,1,0:T(8,128)(2,1)} %param.3), kind=kOutput, calls=%fused_computation.70 | convolution fusion | flops 2148532224 | bytes 27262976 | tf_op jit(solution)/shard_map/ptx,pxi->pti/dot_general | solution.py:87
  747.4 11.2 %add_bitcast_fusion = f32[1,8,1024,128]{2,3,1,0:T(8,128)} fusion(f32[8,128,1024]{2,1,0:T(8,128)} %fusion, bf16[8,1024,128]{2,1,0:T(8,128)(2,1)S(1)} %bitcast.244, bf16[2,8,1024,1024]{3,2,1,0:T(8,128)(2,1)} %param.3), kind=kOutput, calls=%fused_computation.69 | convolution fusion | flops 2148532224 | bytes 27262976 | tf_op jit(solution)/shard_map/ptx,pxi->pti/dot_general | solution.py:92
  773.2 48.3 %psum.47 = f32[]{:T(128)} all-reduce(f32[]{:T(128)} %fusion.40), channel_id=1, replica_groups=mesh['grp'=2,'freq'=16] {'freq'}, use_global_device_ids=true, to_apply=%region_11.12 | all-reduce | flops 1 | bytes 8 | tf_op jit(solution)/shard_map/psum | solution.py:24
  (60 shorter events, 164.4 us)
Async XLA Ops:
  154.5 4.4 copy-start.4
  206.5 10.7 %copy-start = (f32[256,8192]{1,0:T(8,128)S(1)}, f32[256,8192]{1,0:T(8,128)}, u32[]{:S(2)}) copy-start(f32[256,8192]{1,0:T(8,128)} %get-tuple-element.25) | copy-start | bytes 25165828
  229.2 82.0 %all-to-all-start.1 = ((bf16[2,128,64,128]{3,2,0,1:T(8,128)(2,1)}), bf16[2,128,64,128]{3,2,0,1:T(8,128)(2,1)}, u32[]{:S(2)}, u32[]{:S(2)}) async-start(bf16[2,128,64,128]{3,2,0,1:T(8,128)(2,1)} %pad_maximum_fusion.1), calls=%async_computation.1 | async-start | bytes 8388608 | tf_op jit(solution)/shard_map/all_to_all | solution.py:82
  346.5 10.8 %copy-start.2 = (bf16[1,8,16,64,128]{4,3,2,1,0:T(8,128)(2,1)S(1)}, bf16[1,8,16,64,128]{4,3,2,1,0:T(8,128)(2,1)}, u32[]{:S(2)}) copy-start(bf16[1,8,16,64,128]{4,3,2,1,0:T(8,128)(2,1)} %copy.89) | copy-start | bytes 6291460
  374.9 3.2 copy-start.1
  543.4 5.7 slice-start
  544.6 4.5 slice-start.1
  619.1 82.0 %all-to-all-start.3 = ((bf16[2,128,64,128]{3,2,0,1:T(8,128)(2,1)}), bf16[2,128,64,128]{3,2,0,1:T(8,128)(2,1)}, u32[]{:S(2)}, u32[]{:S(2)}) async-start(bf16[2,128,64,128]{3,2,0,1:T(8,128)(2,1)} %pad_maximum_fusion.3), calls=%async_computation.3 | async-start | bytes 8388608 | tf_op jit(solution)/shard_map/all_to_all | solution.py:82
  736.7 10.7 %copy-start.3 = (bf16[1,8,16,64,128]{4,3,2,1,0:T(8,128)(2,1)S(1)}, bf16[1,8,16,64,128]{4,3,2,1,0:T(8,128)(2,1)}, u32[]{:S(2)}) copy-start(bf16[1,8,16,64,128]{4,3,2,1,0:T(8,128)(2,1)} %copy.111) | copy-start | bytes 6291460
where the time goes:
time: 836 us; the launch traced here: 832 us
  blocking collectives  328 us (39%)
  matrix products  244 us (29%)
  waiting for transfers between devices  138 us (17%)
  local copies, waits for them, and re-layouts  60.7 us (7%)
  other arithmetic  47.7 us (6%)
  starting transfers between devices  9.31 us (1%)
    all_to_all x2, blocking collectives, apply_adjoint(): lax.all_to_all(image, 'freq', split_axis=2, concat_axis=1, tiled=True)  211 us
    all_to_all x2, waiting for transfers between devices, body(): lax.all_to_all(spectrum, 'freq', split_axis=1, concat_axis=2, tiled=True)  138 us
    psum x3, blocking collectives, joint_total(): return lax.psum((first, second, third), 'freq')  117 us
    unnamed x22, local copies, waits for them, and re-layouts  31.8 us
    dot_general x2, matrix products, body(): jnp.einsum('ptx,pxi->pti', kernel_imaginary, solution_real, preferred_ele...  28.3 us
    dot_general x2, matrix products, body(): jnp.einsum('ptx,pxi->pti', kernel_imaginary, solution_imaginary, preferre...  28 us
    dot_general x2, matrix products, invert(): jnp.dot(sin_tab.T, widened[1].reshape(NF, -1), precision=highest)  23.4 us
    dot_general x2, matrix products, body(): jnp.einsum('ptx,pxi->pti', kernel_real, solution_imaginary, preferred_ele...  22.4 us
  transfers between devices with their start and end apart: 2, of which 2 were waited for; matrix products, arithmetic and copies ran while one was open for 2% of the time, Pallas kernels for 0%

commit v1 on v0

--- a/solution.py
+++ b/solution.py
@@ -79,8 +79,11 @@
             .reshape(2, NF, rec_local, focal_count)
             .astype(jnp.bfloat16)
         )
-        multiply_block_in = lax.all_to_all(
-            spectrum, "freq", split_axis=1, concat_axis=2, tiled=True
+        multiply_block_in = jnp.concatenate(
+            lax.all_to_all(
+                jnp.stack(jnp.split(spectrum, lax.axis_size("freq"), axis=1)), "freq", 0, 0
+            ),
+            axis=2,
         )
         solution_real = multiply_block_in[0]
         solution_imaginary = multiply_block_in[1]

time: 836 us -> 850 us (1.017)
  local copies, waits for them, and re-layouts: 60.7 us -> 80.6 us
    unnamed x22 -> x51, local copies, waits for them, and re-layouts: 31.8 us -> 54.8 us
where the time goes in v1:
time: 850 us; the launch traced here: 846 us
  blocking collectives  328 us (39%)
  matrix products  243 us (29%)
  waiting for transfers between devices  138 us (16%)
  local copies, waits for them, and re-layouts  80.6 us (9%)
  other arithmetic  43.1 us (5%)
  starting transfers between devices  9.31 us (1%)
    all_to_all x2, blocking collectives, apply_adjoint(): lax.all_to_all(image, 'freq', split_axis=2, concat_axis=1, tiled=True)  211 us
    all_to_all x2, waiting for transfers between devices, body(): lax.all_to_all(jnp.stack(jnp.split(spectrum, lax.axis_size('freq'), axis=...  138 us
    psum x3, blocking collectives, joint_total(): return lax.psum((first, second, third), 'freq')  117 us
    unnamed x51, local copies, waits for them, and re-layouts  54.8 us
    dot_general x2, matrix products, body(): jnp.einsum('ptx,pxi->pti', kernel_imaginary, solution_real, preferred_ele...  28.1 us
    dot_general x2, matrix products, body(): jnp.einsum('ptx,pxi->pti', kernel_imaginary, solution_imaginary, preferre...  26.9 us
    dot_general x2, matrix products, invert(): jnp.dot(sin_tab.T, widened[1].reshape(NF, -1), precision=highest)  23.4 us
    dot_general x2, matrix products, body(): jnp.einsum('ptx,pxi->pti', kernel_real, solution_imaginary, preferred_ele...  22.4 us
  transfers between devices with their start and end apart: 2, of which 2 were waited for; matrix products, arithmetic and copies ran while one was open for 2% of the time, Pallas kernels for 0%

profile of v1, /device:TPU:0, one launch (start us, length us, event | category | flops | bytes accessed | tf_op | source)
XLA Modules:
  0.0 846.3 jit_solution(6757761371329259270)
XLA Ops:
  8.5 10.8 %fusion.14 = f32[8,1024,128]{2,1,0:T(8,128)} fusion(bf16[2,8,1024,1024]{3,2,1,0:T(8,128)(2,1)} %param.3, bf16[2,8,1024,128]{3,2,1,0:T(8,128)(2,1)S(1)} %get-tuple-element.15), kind=kOutput, calls=%fused_computation.14 | convolution fusion | flops 2147483648 | bytes 23068672 | tf_op jit(solution)/shard_map/hvi,hvg->hig/dot_general | solution.py:51
  19.4 10.7 %fusion.12 = f32[8,1024,128]{2,1,0:T(8,128)} fusion(bf16[2,8,1024,1024]{3,2,1,0:T(8,128)(2,1)} %param.3, bf16[2,8,1024,128]{3,2,1,0:T(8,128)(2,1)S(1)} %get-tuple-element.15), kind=kOutput, calls=%fused_computation.12 | convolution fusion | flops 2147483648 | bytes 23068672 | tf_op jit(solution)/shard_map/hvi,hvg->hig/dot_general | solution.py:56
  39.7 10.4 %fusion.68 = bf16[1,8,1024,128]{3,2,1,0:T(8,128)(2,1)S(1)} fusion(f32[8,1024,128]{2,1,0:T(8,128)} %fusion.12, bf16[2,8,1024,128]{3,2,1,0:T(8,128)(2,1)S(1)} %get-tuple-element.15, bf16[2,8,1024,1024]{3,2,1,0:T(8,128)(2,1)} %param.3), kind=kOutput, calls=%fused_computation.98 | convolution fusion | flops 2149580800 | bytes 25165824 | tf_op jit(solution)/shard_map/hvi,hvg->hig/dot_general | solution.py:54
  53.2 99.3 %all_to_all.40 = bf16[2,8,1024,128]{3,1,0,2:T(8,128)(2,1)S(1)} all-to-all(bf16[2,8,1024,128]{3,1,0,2:T(8,128)(2,1)S(1)} %copy.82), channel_id=1, replica_groups=mesh['grp'=2,'freq'=16] {'freq'}, dimensions={2} | all-to-all | bytes 8388608 | tf_op jit(solution)/shard_map/all_to_all | solution.py:60
  159.0 12.1 %multiply_reduce_fusion.4 = (f32[]{:T(128)}, f32[256,8192]{1,0:T(8,128)}) fusion(s32[8192]{0:T(1024)S(1)} %bitcast.367, f32[256,8192]{1,0:T(8,128)S(1)} %fusion.78, bf16[16,8,64,128]{3,2,1,0:T(8,128)(2,1)S(1)} %get-tuple-element.22), kind=kOutput, calls=%fused_computation.58 | convolution fusion | flops 3232202752 | bytes 18907140 | tf_op jit(solution)/shard_map/dot_general | solution.py:40
  171.1 34.1 %all-reduce.1 = (f32[]{:T(128)}, f32[]{:T(128)}) all-reduce(f32[]{:T(128)} %get-tuple-element.24, f32[]{:T(128)} %get-tuple-element.14), channel_id=1, replica_groups=mesh['grp'=2,'freq'=16] {'freq'}, use_global_device_ids=true, to_apply=%region_1.2 | all-reduce | flops 2 | bytes 16 | tf_op jit(solution)/shard_map/psum | solution.py:24
  206.5 10.7 %fusion.94 = bf16[16,8,64,128]{3,1,2,0:T(8,128)(2,1)S(1)} fusion(s32[8192]{0:T(1024)S(1)} %bitcast.368, f32[256,8192]{1,0:T(8,128)} %get-tuple-element.25, f32[]{:T(128)S(6)} %mul.210), kind=kOutput, calls=%fused_computation.126 | convolution fusion | flops 3232202752 | bytes 10518532 | tf_op jit(solution)/shard_map/dot_general | solution.py:76
  251.2 68.8 %all-to-all-done.1 = bf16[16,2,8,64,128]{4,3,2,1,0:T(8,128)(2,1)} async-done(((bf16[16,2,8,64,128]{4,3,2,1,0:T(8,128)(2,1)}), bf16[16,2,8,64,128]{4,3,2,1,0:T(8,128)(2,1)}, u32[]{:S(2)}, u32[]{:S(2)}) %all-to-all-start.1) | async-done | bytes 4194336 | tf_op jit(solution)/shard_map/all_to_all | solution.py:83
  325.5 13.4 %fusion.10 = f32[8,128,1024]{2,1,0:T(8,128)} fusion(bf16[8,1024,128]{2,1,0:T(8,128)(2,1)S(1)} %bitcast.359, bf16[2,8,1024,1024]{3,2,1,0:T(8,128)(2,1)} %param.3), kind=kOutput, calls=%fused_computation.10 | convolution fusion | flops 2147483648 | bytes 23068672 | tf_op jit(solution)/shard_map/ptx,pxi->pti/dot_general | solution.py:92
  338.9 14.0 %fusion.8 = f32[8,128,1024]{2,1,0:T(8,128)} fusion(bf16[8,1024,128]{2,1,0:T(8,128)(2,1)} %bitcast.363, bf16[2,8,1024,1024]{3,2,1,0:T(8,128)(2,1)} %param.3), kind=kOutput, calls=%fused_computation.8 | convolution fusion | flops 2147483648 | bytes 23068672 | tf_op jit(solution)/shard_map/ptx,pxi->pti/dot_general | solution.py:97
  352.9 10.7 %subtract_bitcast_fusion.1 = f32[1,8,1024,128]{2,3,1,0:T(8,128)S(1)} fusion(f32[8,128,1024]{2,1,0:T(8,128)} %fusion.10, bf16[8,1024,128]{2,1,0:T(8,128)(2,1)} %bitcast.364, bf16[2,8,1024,1024]{3,2,1,0:T(8,128)(2,1)} %param.3), kind=kOutput, calls=%fused_computation.74 | convolution fusion | flops 2148532224 | bytes 27262976 | tf_op jit(solution)/shard_map/ptx,pxi->pti/dot_general | solution.py:90
  363.6 11.2 %add_bitcast_fusion.1 = f32[1,8,1024,128]{2,3,1,0:T(8,128)} fusion(f32[8,128,1024]{2,1,0:T(8,128)} %fusion.8, bf16[8,1024,128]{2,1,0:T(8,128)(2,1)S(1)} %bitcast.360, bf16[2,8,1024,1024]{3,2,1,0:T(8,128)(2,1)} %param.3), kind=kOutput, calls=%fused_computation.73 | convolution fusion | flops 2148532224 | bytes 27262976 | tf_op jit(solution)/shard_map/ptx,pxi->pti/dot_general | solution.py:95
  385.1 10.1 %fusion.6 = f32[8,128,1024]{2,1,0:T(8,128)} fusion(bf16[2,8,1024,1024]{3,2,1,0:T(8,128)(2,1)} %param.3, bf16[2,8,1024,128]{2,3,1,0:T(8,128)(2,1)S(1)} %convert_element_type.32), kind=kOutput, calls=%fused_computation.6 | convolution fusion | flops 2147483648 | bytes 23068672 | tf_op jit(solution)/shard_map/hvi,hvg->hig/dot_general | solution.py:51
  395.2 10.1 %fusion.4 = f32[8,128,1024]{2,1,0:T(8,128)} fusion(bf16[2,8,1024,1024]{3,2,1,0:T(8,128)(2,1)} %param.3, bf16[2,8,1024,128]{2,3,1,0:T(8,128)(2,1)S(1)} %convert_element_type.32), kind=kOutput, calls=%fused_computation.4 | convolution fusion | flops 2147483648 | bytes 23068672 | tf_op jit(solution)/shard_map/hvi,hvg->hig/dot_general | solution.py:56
  414.8 10.8 %fusion.70 = bf16[1,8,1024,128]{2,3,1,0:T(8,128)(2,1)} fusion(f32[8,128,1024]{2,1,0:T(8,128)} %fusion.4, bf16[2,8,1024,1024]{3,2,1,0:T(8,128)(2,1)} %param.3, bf16[2,8,1024,128]{2,3,1,0:T(8,128)(2,1)S(1)} %convert_element_type.32), kind=kOutput, calls=%fused_computation.100 | convolution fusion | flops 2149580800 | bytes 25165824 | tf_op jit(solution)/shard_map/hvi,hvg->hig/dot_general | solution.py:54
  436.5 112.1 %all_to_all.41 = bf16[2,8,1024,128]{3,1,0,2:T(8,128)(2,1)S(1)} all-to-all(bf16[2,8,1024,128]{3,1,0,2:T(8,128)(2,1)} %copy.98), channel_id=1, replica_groups=mesh['grp'=2,'freq'=16] {'freq'}, dimensions={2} | all-to-all | bytes 8388608 | tf_op jit(solution)/shard_map/all_to_all | solution.py:60
  556.0 11.4 %multiply_reduce_fusion = (f32[]{:T(128)}, f32[]{:T(128)}, f32[256,8192]{1,0:T(8,128)}) fusion(s32[8192]{0:T(1024)S(1)} %bitcast.370, f32[]{:T(128)S(6)} %mul.210, f32[256,8192]{1,0:T(8,128)S(1)} %bitcast.348, f32[256,8192]{1,0:T(8,128)S(1)} %fusion.73, bf16[16,8,64,128]{3,2,1,0:T(8,128)(2,1)S(1)} %get-tuple-element.27), kind=kOutput, calls=%fused_computation.53 | convolution fusion | flops 3240591360 | bytes 27295756 | tf_op jit(solution)/shard_map/dot_general | solution.py:40
  567.3 34.2 %all-reduce = (f32[]{:T(128)}, f32[]{:T(128)}, f32[]{:T(128)}) all-reduce(f32[]{:T(128)} %get-tuple-element.12, f32[]{:T(128)} %get-tuple-element.6, f32[]{:T(128)} %get-tuple-element.5), channel_id=1, replica_groups=mesh['grp'=2,'freq'=16] {'freq'}, use_global_device_ids=true, to_apply=%region_5.6 | all-reduce | flops 3 | bytes 24 | tf_op jit(solution)/shard_map/psum | solution.py:24
  648.6 69.0 %all-to-all-done.3 = bf16[16,2,8,64,128]{4,3,2,1,0:T(8,128)(2,1)} async-done(((bf16[16,2,8,64,128]{4,3,2,1,0:T(8,128)(2,1)}), bf16[16,2,8,64,128]{4,3,2,1,0:T(8,128)(2,1)}, u32[]{:S(2)}, u32[]{:S(2)}) %all-to-all-start.3) | async-done | bytes 4194336 | tf_op jit(solution)/shard_map/all_to_all | solution.py:83
  723.1 13.4 %fusion.2 = f32[8,128,1024]{2,1,0:T(8,128)} fusion(bf16[8,1024,128]{2,1,0:T(8,128)(2,1)S(1)} %bitcast.361, bf16[2,8,1024,1024]{3,2,1,0:T(8,128)(2,1)} %param.3), kind=kOutput, calls=%fused_computation.2 | convolution fusion | flops 2147483648 | bytes 23068672 | tf_op jit(solution)/shard_map/ptx,pxi->pti/dot_general | solution.py:92
  736.5 14.1 %fusion = f32[8,128,1024]{2,1,0:T(8,128)} fusion(bf16[8,1024,128]{2,1,0:T(8,128)(2,1)} %bitcast.365, bf16[2,8,1024,1024]{3,2,1,0:T(8,128)(2,1)} %param.3), kind=kOutput, calls=%fused_computation | convolution fusion | flops 2147483648 | bytes 23068672 | tf_op jit(solution)/shard_map/ptx,pxi->pti/dot_general | solution.py:97
  750.6 10.8 %subtract_bitcast_fusion = f32[1,8,1024,128]{2,3,1,0:T(8,128)S(1)} fusion(f32[8,128,1024]{2,1,0:T(8,128)} %fusion.2, bf16[8,1024,128]{2,1,0:T(8,128)(2,1)} %bitcast.366, bf16[2,8,1024,1024]{3,2,1,0:T(8,128)(2,1)} %param.3), kind=kOutput, calls=%fused_computation.70 | convolution fusion | flops 2148532224 | bytes 27262976 | tf_op jit(solution)/shard_map/ptx,pxi->pti/dot_general | solution.py:90
  761.4 11.2 %add_bitcast_fusion = f32[1,8,1024,128]{2,3,1,0:T(8,128)} fusion(f32[8,128,1024]{2,1,0:T(8,128)} %fusion, bf16[8,1024,128]{2,1,0:T(8,128)(2,1)S(1)} %bitcast.362, bf16[2,8,1024,1024]{3,2,1,0:T(8,128)(2,1)} %param.3), kind=kOutput, calls=%fused_computation.69 | convolution fusion | flops 2148532224 | bytes 27262976 | tf_op jit(solution)/shard_map/ptx,pxi->pti/dot_general | solution.py:95
  787.1 48.3 %psum.47 = f32[]{:T(128)} all-reduce(f32[]{:T(128)} %fusion.40), channel_id=1, replica_groups=mesh['grp'=2,'freq'=16] {'freq'}, use_global_device_ids=true, to_apply=%region_11.12 | all-reduce | flops 1 | bytes 8 | tf_op jit(solution)/shard_map/psum | solution.py:24
  (82 shorter events, 179.6 us)
Async XLA Ops:
  154.5 4.4 copy-start.2
  206.5 10.7 %copy-start = (f32[256,8192]{1,0:T(8,128)S(1)}, f32[256,8192]{1,0:T(8,128)}, u32[]{:S(2)}) copy-start(f32[256,8192]{1,0:T(8,128)} %get-tuple-element.25) | copy-start | bytes 25165828
  238.0 82.0 %all-to-all-start.1 = ((bf16[16,2,8,64,128]{4,3,2,1,0:T(8,128)(2,1)}), bf16[16,2,8,64,128]{4,3,2,1,0:T(8,128)(2,1)}, u32[]{:S(2)}, u32[]{:S(2)}) async-start(bf16[16,2,8,64,128]{4,3,2,1,0:T(8,128)(2,1)} %fusion.121), calls=%async_computation.1 | async-start | bytes 8388608 | tf_op jit(solution)/shard_map/all_to_all | solution.py:83
  381.2 3.2 copy-start.1
  550.6 5.3 slice-start
  551.7 4.3 slice-start.1
  635.4 82.2 %all-to-all-start.3 = ((bf16[16,2,8,64,128]{4,3,2,1,0:T(8,128)(2,1)}), bf16[16,2,8,64,128]{4,3,2,1,0:T(8,128)(2,1)}, u32[]{:S(2)}, u32[]{:S(2)}) async-start(bf16[16,2,8,64,128]{4,3,2,1,0:T(8,128)(2,1)} %fusion.105), calls=%async_computation.3 | async-start | bytes 8388608 | tf_op jit(solution)/shard_map/all_to_all | solution.py:83
